TPU v7x, 32 devices: a whole 2x2x4 slice. The times are simulated.
32 devices in a mesh: dp: 2 (over x), lat: 4 (over y, core), lon: 4 (over z).
Axes of the slice: x: 2, y: 2, z: 4, core: 2. Of those that a mesh axis runs over, the one named last changes fastest.
Arguments:
- hidden_in: bfloat16 [2, 64, 512, 128], P('dp', 'lat', 'lon'), may hold values from -6 to 6
- conv_weight: bfloat16 [3, 3, 128, 128], replicated, may hold values from -0.1875 to 0.1875
- conv_bias: float32 [128], replicated, may hold values from -3 to 3
- proj_weight: float32 [128], replicated, may hold values from -5 to 5
- ocean_depth: float32 [64, 512], P('lat', 'lon'), may hold values from 0.5 to 2
- sea_mask: int32 [64, 512], P('lat', 'lon'), may hold values 0 or 1
- step_alpha: float32 [6], replicated, may hold values from 0.04 to 0.07
- step_beta: float32 [6], replicated, may hold values from 0.1 to 0.5
- surface_cotangent: float32 [2, 64, 512], P('dp', 'lat', 'lon'), may hold values from -20 to 20
Outputs:
- grad_hidden: bfloat16 [2, 64, 512, 128], P('dp', 'lat', 'lon')
- grad_weight: float32 [128, 3, 3, 128], P(('lat', 'lon'))
- grad_bias: float32 [128], replicated
- grad_proj: float32 [128], replicated
All inputs are finite; a program needn't handle non-finite values. No bound on the sum of `sea_mask` on one device may be relied on, other than what follows from the above.
Results may differ from a plain program's by a relative error of at most 0.01.
Values may be sent and summed in bfloat16 or wider, within the bound.
A program may use at most 64 MiB of HBM per device.

v0:
```python
import math
import jax
import jax.numpy as jnp
from jax import lax
from jax.sharding import PartitionSpec as P

ITERS = 6
helm_coef = 0.5


def extended(cells, sides, width, closed):
    for axis, dim in sides:
        count = lax.axis_size(axis)
        ends = count if closed else count - 1
        head = lax.slice_in_dim(cells, 0, width, axis=dim)
        tail = lax.slice_in_dim(cells, cells.shape[dim] - width, cells.shape[dim], axis=dim)
        cells = jnp.concatenate(
            [
                lax.ppermute(tail, axis, [(i, (i + 1) % count) for i in range(ends)]),
                cells,
                lax.ppermute(head, axis, [((i + 1) % count, i) for i in range(ends)]),
            ],
            axis=dim,
        )
    return cells


def operate(field_ext, mask_ext, depth_ext):
    rows_in = field_ext.shape[-2] - 2
    cols_in = field_ext.shape[-1] - 2
    center = field_ext[..., 1:-1, 1:-1]
    mask_mid = mask_ext[1:-1, 1:-1]
    depth_mid = depth_ext[1:-1, 1:-1]
    result = helm_coef * center
    for row_off, col_off in ((0, 1), (2, 1), (1, 0), (1, 2)):
        beside = field_ext[..., row_off : row_off + rows_in, col_off : col_off + cols_in]
        mask_near = mask_ext[row_off : row_off + rows_in, col_off : col_off + cols_in]
        depth_near = depth_ext[row_off : row_off + rows_in, col_off : col_off + cols_in]
        weight = mask_near * 0.5 * (depth_mid + depth_near)
        result = result + weight * (center - beside)
    return mask_mid * result


def solve_steps(adjoint_start, mask_ext, depth_ext, step_alpha, step_beta, widen):
    solution = jnp.zeros_like(adjoint_start)
    residual = adjoint_start
    direction = adjoint_start
    for turn_index in range(ITERS):
        solution = solution + step_alpha[turn_index] * direction
        if turn_index + 1 < ITERS:
            applied = operate(widen(direction), mask_ext, depth_ext)
            residual = residual - step_alpha[turn_index] * applied
            direction = residual + step_beta[turn_index] * direction
    return solution


def halo_field(field):
    field = extended(field, (("lat", 1),), 1, False)
    return extended(field, (("lon", 2),), 1, True)


def shards(
    hidden_in,
    conv_weight,
    conv_bias,
    proj_weight,
    ocean_depth,
    sea_mask,
    step_alpha,
    step_beta,
    surface_cotangent,
):
    samples, lat_rows, lon_cols, channels = hidden_in.shape
    mask_float = sea_mask.astype(jnp.float32)
    counted, summed = lax.psum(
        (jnp.sum(mask_float), jnp.sum(mask_float * surface_cotangent, axis=(1, 2))), ("lat", "lon")
    )
    adjoint_start = mask_float * (surface_cotangent - (summed / counted)[:, None, None])
    coefs = jnp.stack([mask_float, ocean_depth])
    coefs = extended(coefs, (("lat", 1),), 1, False)
    coefs = extended(coefs, (("lon", 2),), 1, True)
    solution = solve_steps(adjoint_start, coefs[0], coefs[1], step_alpha, step_beta, halo_field)
    forcing_grad = mask_float * solution
    padded = extended(hidden_in, (("lat", 1),), 1, False)
    padded = extended(padded, (("lon", 2),), 1, True)
    cell_count = samples * lat_rows * lon_cols
    shifted = [
        padded[:, row_off : row_off + lat_rows, col_off : col_off + lon_cols, :].reshape(
            cell_count, channels
        )
        for row_off in range(3)
        for col_off in range(3)
    ]
    preact = conv_bias
    for offset in range(9):
        preact = preact + jnp.dot(
            shifted[offset],
            conv_weight[offset // 3, offset % 3],
            preferred_element_type=jnp.float32,
        )
    sigma = jax.nn.sigmoid(preact)
    active = preact * sigma
    slope_act = sigma * (1.0 + preact * (1.0 - sigma))
    force_col = forcing_grad.reshape(cell_count)[:, None]
    grad_pre = (force_col * proj_weight * slope_act).astype(jnp.bfloat16)
    local_proj = jnp.sum(active * force_col, axis=0)
    local_bias = jnp.sum(grad_pre.astype(jnp.float32), axis=0)
    grad_ext = extended(
        grad_pre.reshape(samples, lat_rows, lon_cols, channels), (("lat", 1),), 1, False
    )
    grad_ext = extended(grad_ext, (("lon", 2),), 1, True)
    backed = jnp.zeros((cell_count, channels), jnp.float32)
    for row_off in range(3):
        for col_off in range(3):
            window = grad_ext[
                :, 2 - row_off : 2 - row_off + lat_rows, 2 - col_off : 2 - col_off + lon_cols, :
            ].reshape(cell_count, channels)
            backed = backed + lax.dot_general(
                window,
                conv_weight[row_off, col_off],
                (((1,), (1,)), ((), ())),
                preferred_element_type=jnp.float32,
            )
    grad_hidden = backed.reshape(samples, lat_rows, lon_cols, channels).astype(jnp.bfloat16)
    share = channels // lax.axis_size(("lat", "lon"))
    blocks = []
    for shifted_cols in shifted:
        blocks.append(
            lax.dot_general(
                shifted_cols, grad_pre, (((0,), (0,)), ((), ())), preferred_element_type=jnp.float32
            )
        )
    spatial = lax.psum_scatter(
        jnp.stack(blocks, axis=1).reshape(share * lax.axis_size(("lat", "lon")), 3, 3, channels),
        ("lat", "lon"),
        scatter_dimension=0,
        tiled=True,
    )
    own_weight = lax.psum(spatial, "dp")
    total_bias, total_proj = lax.psum((local_bias, local_proj), ("dp", "lat", "lon"))
    all_cells = cell_count * lax.axis_size("dp") * lax.axis_size("lat") * lax.axis_size("lon")
    grad_scale = 1.0 / math.sqrt(all_cells)
    return (grad_hidden, own_weight * grad_scale, total_bias * grad_scale, total_proj * grad_scale)


def solution(mesh):
    in_specs = (
        P("dp", "lat", "lon", None),
        P(),
        P(),
        P(),
        P("lat", "lon"),
        P("lat", "lon"),
        P(),
        P(),
        P("dp", "lat", "lon"),
    )
    out_specs = (P("dp", "lat", "lon", None), P(("lat", "lon"), None, None, None), P(), P())
    return jax.shard_map(shards, mesh=mesh, in_specs=in_specs, out_specs=out_specs, check_vma=False)
```

profile of v0, /device:TPU:0, one launch (start us, length us, event | category | flops | bytes accessed | tf_op | source)
XLA Modules:
  0.0 225.2 jit_solution(6670252528962750081)
XLA Ops:
  8.7 2.4 %collective-permute-start = (f32[2,1,128]{2,1,0:T(1,128)S(1)}, f32[2,1,128]{2,1,0:T(1,128)S(1)}, u32[]{:S(2)}, u32[]{:S(2)}) collective-permute-start(f32[2,1,128]{2,1,0:T(1,128)S(1)} %get-tuple-element.57), channel_id=1, source_target_pairs={{0,4},{4,8},{8,12},{1,5},{5,9},{9,13},{2,6},{6,10},{10,14},{3,7},{... | collective-permute-start | bytes 3080 | tf_op jit(solution)/shard_map/ppermute | solution.py:19
  11.1 1.3 collective-permute-start.1
  12.4 1.3 convert_reduce_fusion.1
  13.7 1.3 multiply_reduce_fusion.1
  15.0 36.6 %all-reduce.1 = (f32[1]{0:T(128)}, f32[1]{0:T(128)}) all-reduce(f32[1]{0:T(128)} %bitcast.2, f32[1]{0:T(128)} %bitcast.3), channel_id=1, replica_groups=mesh['dp'=2,'lat'=4,'lon'=4] {'lat','lon'}, use_global_device_ids=true, to_apply=%region_1.0 | all-reduce | flops 2 | bytes 16 | tf_op jit(solution)/shard_map/psum | solution.py:75
  53.6 1.3 collective-permute-start.4
  54.9 1.3 collective-permute-start.5
  56.2 1.5 fusion.171
  57.8 1.5 fusion.172
  61.0 3.7 %collective-permute-start.3 = (f32[2,18,1]{2,1,0:T(8,128)S(1)}, f32[2,18,1]{2,1,0:T(8,128)S(1)}, u32[]{:S(2)}, u32[]{:S(2)}) collective-permute-start(f32[2,18,1]{2,1,0:T(8,128)S(1)} %get-tuple-element.56), channel_id=1, source_target_pairs={{1,0},{2,1},{3,2},{0,3},{5,4},{6,5},{7,6},{4,7},{9,8},{10,9},{11,1... | collective-permute-start | bytes 440 | tf_op jit(solution)/shard_map/ppermute | solution.py:21
  64.7 2.0 collective-permute-start.7
  68.4 1.3 multiply_add_fusion.3
  69.7 2.6 %collective-permute-start.8 = (f32[1,1,128]{2,1,0:T(1,128)S(1)}, f32[1,1,128]{2,1,0:T(1,128)S(1)}, u32[]{:S(2)}, u32[]{:S(2)}) collective-permute-start(f32[1,1,128]{2,1,0:T(1,128)S(1)} %get-tuple-element.75), channel_id=1, source_target_pairs={{0,4},{4,8},{8,12},{1,5},{5,9},{9,13},{2,6},{6,10},{10,14},{3,7},{... | collective-permute-start | bytes 1544 | tf_op jit(solution)/shard_map/ppermute | solution.py:19
  72.3 1.3 collective-permute-start.9
  73.6 4.7 %collective-permute-done.9 = f32[1,1,128]{2,1,0:T(1,128)S(1)} collective-permute-done((f32[1,1,128]{2,1,0:T(1,128)S(1)}, f32[1,1,128]{2,1,0:T(1,128)S(1)}, u32[]{:S(2)}, u32[]{:S(2)}) %collective-permute-start.9) | collective-permute-done | bytes 544 | tf_op jit(solution)/shard_map/ppermute | solution.py:21
  78.4 3.8 %collective-permute-start.11 = (f32[1,18,1]{2,1,0:T(8,128)S(1)}, f32[1,18,1]{2,1,0:T(8,128)S(1)}, u32[]{:S(2)}, u32[]{:S(2)}) collective-permute-start(f32[1,18,1]{2,1,0:T(8,128)S(1)} %get-tuple-element.66), channel_id=1, source_target_pairs={{1,0},{2,1},{3,2},{0,3},{5,4},{6,5},{7,6},{4,7},{9,8},{10,9},{11,1... | collective-permute-start | bytes 224 | tf_op jit(solution)/shard_map/ppermute | solution.py:21
  82.2 1.7 collective-permute-done.10
  83.9 1.3 multiply_add_fusion.2
  85.2 3.3 %collective-permute-start.12 = (f32[1,1,128]{2,1,0:T(1,128)S(1)}, f32[1,1,128]{2,1,0:T(1,128)S(1)}, u32[]{:S(2)}, u32[]{:S(2)}) collective-permute-start(f32[1,1,128]{2,1,0:T(1,128)S(1)} %get-tuple-element.73), channel_id=1, source_target_pairs={{0,4},{4,8},{8,12},{1,5},{5,9},{9,13},{2,6},{6,10},{10,14},{3,7},{... | collective-permute-start | bytes 1544 | tf_op jit(solution)/shard_map/ppermute | solution.py:19
  88.6 1.3 collective-permute-start.13
  89.9 2.2 collective-permute-done.13
  93.3 2.8 %collective-permute-start.15 = (f32[1,18,1]{2,1,0:T(8,128)S(1)}, f32[1,18,1]{2,1,0:T(8,128)S(1)}, u32[]{:S(2)}, u32[]{:S(2)}) collective-permute-start(f32[1,18,1]{2,1,0:T(8,128)S(1)} %get-tuple-element.64), channel_id=1, source_target_pairs={{1,0},{2,1},{3,2},{0,3},{5,4},{6,5},{7,6},{4,7},{9,8},{10,9},{11,1... | collective-permute-start | bytes 224 | tf_op jit(solution)/shard_map/ppermute | solution.py:21
  96.1 1.6 collective-permute-done.14
  97.7 1.4 multiply_add_fusion.1
  99.0 3.4 %collective-permute-start.16 = (f32[1,1,128]{2,1,0:T(1,128)S(1)}, f32[1,1,128]{2,1,0:T(1,128)S(1)}, u32[]{:S(2)}, u32[]{:S(2)}) collective-permute-start(f32[1,1,128]{2,1,0:T(1,128)S(1)} %get-tuple-element.71), channel_id=1, source_target_pairs={{0,4},{4,8},{8,12},{1,5},{5,9},{9,13},{2,6},{6,10},{10,14},{3,7},{... | collective-permute-start | bytes 1544 | tf_op jit(solution)/shard_map/ppermute | solution.py:19
  102.4 1.3 collective-permute-start.17
  103.7 2.2 collective-permute-done.17
  106.0 1.3 collective-permute-start.18
  107.3 2.6 %collective-permute-start.19 = (f32[1,18,1]{2,1,0:T(8,128)S(1)}, f32[1,18,1]{2,1,0:T(8,128)S(1)}, u32[]{:S(2)}, u32[]{:S(2)}) collective-permute-start(f32[1,18,1]{2,1,0:T(8,128)S(1)} %get-tuple-element.62), channel_id=1, source_target_pairs={{1,0},{2,1},{3,2},{0,3},{5,4},{6,5},{7,6},{4,7},{9,8},{10,9},{11,1... | collective-permute-start | bytes 224 | tf_op jit(solution)/shard_map/ppermute | solution.py:21
  109.9 1.6 collective-permute-done.18
  111.5 1.3 multiply_add_fusion
  112.8 3.4 %collective-permute-start.20 = (f32[1,1,128]{2,1,0:T(1,128)S(1)}, f32[1,1,128]{2,1,0:T(1,128)S(1)}, u32[]{:S(2)}, u32[]{:S(2)}) collective-permute-start(f32[1,1,128]{2,1,0:T(1,128)S(1)} %get-tuple-element.69), channel_id=1, source_target_pairs={{0,4},{4,8},{8,12},{1,5},{5,9},{9,13},{2,6},{6,10},{10,14},{3,7},{... | collective-permute-start | bytes 1544 | tf_op jit(solution)/shard_map/ppermute | solution.py:19
  116.2 1.3 collective-permute-start.21
  117.5 3.5 %collective-permute-start.24 = (bf16[1,1,128,128]{3,2,1,0:T(8,128)(2,1)S(1)}, bf16[1,1,128,128]{3,2,1,0:T(8,128)(2,1)S(1)}, u32[]{:S(2)}, u32[]{:S(2)}) collective-permute-start(bf16[1,1,128,128]{3,2,1,0:T(8,128)(2,1)S(1)} %get-tuple-element.52), channel_id=1, source_target_pairs={{0,4},{4,8},{8,12},{1,5},{5,9},{9,13},{2,6},{6,10},{10,14},{3,7},{... | collective-permute-start | bytes 98312 | tf_op jit(solution)/shard_map/ppermute | solution.py:19
  121.0 1.3 collective-permute-start.25
  122.4 1.3 collective-permute-start.22
  123.7 2.6 %collective-permute-start.23 = (f32[1,18,1]{2,1,0:T(8,128)S(1)}, f32[1,18,1]{2,1,0:T(8,128)S(1)}, u32[]{:S(2)}, u32[]{:S(2)}) collective-permute-start(f32[1,18,1]{2,1,0:T(8,128)S(1)} %get-tuple-element.60), channel_id=1, source_target_pairs={{1,0},{2,1},{3,2},{0,3},{5,4},{6,5},{7,6},{4,7},{9,8},{10,9},{11,1... | collective-permute-start | bytes 224 | tf_op jit(solution)/shard_map/ppermute | solution.py:21
  126.3 1.6 collective-permute-done.22
  128.0 4.5 %fusion.69 = f32[2048]{0:T(1024)S(1)} fusion(f32[1,16,128]{2,1,0:T(8,128)S(1)} %get-tuple-element.11, f32[1,16,128]{2,1,0:T(8,128)S(1)} %get-tuple-element.21, f32[1,16,128]{2,1,0:T(8,128)S(1)} %get-tuple-element.10, f32[1,18,1]{2,1,0:T(8,128)S(1)} %collective-permute-done.23, f32[1,1,128]{2,1,0:T(1,128)S(1)} %collective-permute-done.21, ...), kind=kLoop, calls=%fused_computation.128 | loop fusion | flops 79872 | bytes 107692 | tf_op jit(solution)/shard_map/mul | solution.py:105
  132.9 1.4 collective-permute-start.26
  134.2 2.6 %collective-permute-start.27 = (bf16[1,18,1,128]{3,2,1,0:T(2,128)(2,1)S(1)}, bf16[1,18,1,128]{3,2,1,0:T(2,128)(2,1)S(1)}, u32[]{:S(2)}, u32[]{:S(2)}) collective-permute-start(bf16[1,18,1,128]{3,2,1,0:T(2,128)(2,1)S(1)} %get-tuple-element.43), channel_id=1, source_target_pairs={{1,0},{2,1},{3,2},{0,3},{5,4},{6,5},{7,6},{4,7},{9,8},{10,9},{11,1... | collective-permute-start | bytes 13832 | tf_op jit(solution)/shard_map/ppermute | solution.py:21
  137.1 1.3 collective-permute-done.26
  146.9 2.2 collective-permute-start.28
  149.1 1.3 collective-permute-start.29
  150.4 45.0 %all-reduce = (f32[128]{0:T(128)S(1)}, f32[128]{0:T(128)S(1)}) all-reduce(f32[128]{0:T(128)S(1)} %get-tuple-element.8, f32[128]{0:T(128)S(1)} %get-tuple-element.22), channel_id=1, replica_groups=mesh['dp'=2,'lat'=4,'lon'=4] {'dp','lat','lon'}, use_global_device_ids=true, to_apply=%region_7.0 | all-reduce | flops 256 | bytes 2048 | tf_op jit(solution)/shard_map/psum | solution.py:140
  196.0 2.4 %collective-permute-start.30 = (bf16[1,18,1,128]{3,2,1,0:T(2,128)(2,1)S(1)}, bf16[1,18,1,128]{3,2,1,0:T(2,128)(2,1)S(1)}, u32[]{:S(2)}, u32[]{:S(2)}) collective-permute-start(bf16[1,18,1,128]{3,2,1,0:T(2,128)(2,1)S(1)} %get-tuple-element.37), channel_id=1, source_target_pairs={{1,0},{2,1},{3,2},{0,3},{5,4},{6,5},{7,6},{4,7},{9,8},{10,9},{11,1... | collective-permute-start | bytes 13832 | tf_op jit(solution)/shard_map/ppermute | solution.py:21
  199.7 4.1 %collective-permute-done.31 = bf16[1,18,1,128]{3,2,1,0:T(2,128)(2,1)S(1)} collective-permute-done((bf16[1,18,1,128]{3,2,1,0:T(2,128)(2,1)S(1)}, bf16[1,18,1,128]{3,2,1,0:T(2,128)(2,1)S(1)}, u32[]{:S(2)}, u32[]{:S(2)}) %collective-permute-start.31) | collective-permute-done | bytes 4640 | tf_op jit(solution)/shard_map/ppermute | solution.py:19
  207.9 9.9 %psum.37 = f32[8,3,3,128]{3,0,2,1:T(8,128)S(1)} all-reduce(f32[8,3,3,128]{3,0,2,1:T(8,128)} %reduce-scatter.2.cloned.1.call-done), channel_id=1, replica_groups=mesh['dp'=2,'lat'=4,'lon'=4] {'dp'}, use_global_device_ids=true, to_apply=%region_5.0 | all-reduce | flops 9216 | bytes 73728 | tf_op jit(solution)/shard_map/psum | solution.py:139
  (105 shorter events, 22.7 us)
Async XLA Ops:
  7.2 120.8 %copy-start.3 = (s32[16,128]{1,0:T(8,128)S(1)}, s32[16,128]{1,0:T(8,128)}, u32[]{:S(2)}) copy-start(s32[16,128]{1,0:T(8,128)} %param.14) | copy-start | bytes 24580
  7.2 110.3 %copy-start = (bf16[1,16,128,128]{3,2,1,0:T(8,128)(2,1)S(1)}, bf16[1,16,128,128]{3,2,1,0:T(8,128)(2,1)}, u32[]{:S(2)}) copy-start(bf16[1,16,128,128]{3,2,1,0:T(8,128)(2,1)} %param.9) | copy-start | bytes 1572868
  7.2 200.7 %reduce-scatter.2.cloned.1.call-start = ((), (), s32[]{:S(2)}) async-start(), calls=%async_computation.1 | async-start | bytes 626688 | tf_op jit(solution)/shard_map/reduce_scatter | solution.py:133
  8.7 51.3 %collective-permute-start = (f32[2,1,128]{2,1,0:T(1,128)S(1)}, f32[2,1,128]{2,1,0:T(1,128)S(1)}, u32[]{:S(2)}, u32[]{:S(2)}) collective-permute-start(f32[2,1,128]{2,1,0:T(1,128)S(1)} %get-tuple-element.57), channel_id=1, source_target_pairs={{0,4},{4,8},{8,12},{1,5},{5,9},{9,13},{2,6},{6,10},{10,14},{3,7},{... | collective-permute-start | bytes 3080 | tf_op jit(solution)/shard_map/ppermute | solution.py:19
  11.1 49.0 %collective-permute-start.1 = (f32[2,1,128]{2,1,0:T(1,128)S(1)}, f32[2,1,128]{2,1,0:T(1,128)S(1)}, u32[]{:S(2)}, u32[]{:S(2)}) collective-permute-start(f32[2,1,128]{2,1,0:T(1,128)S(1)} %get-tuple-element.58), channel_id=1, source_target_pairs={{4,0},{8,4},{12,8},{5,1},{9,5},{13,9},{6,2},{10,6},{14,10},{7,3},{... | collective-permute-start | bytes 3080 | tf_op jit(solution)/shard_map/ppermute | solution.py:21
  53.6 5.6 %collective-permute-start.4 = (f32[1,1,128]{2,1,0:T(1,128)S(1)}, f32[1,1,128]{2,1,0:T(1,128)S(1)}, u32[]{:S(2)}, u32[]{:S(2)}) collective-permute-start(f32[1,1,128]{2,1,0:T(1,128)S(1)} %get-tuple-element.77), channel_id=1, source_target_pairs={{0,4},{4,8},{8,12},{1,5},{5,9},{9,13},{2,6},{6,10},{10,14},{3,7},{... | collective-permute-start | bytes 1544 | tf_op jit(solution)/shard_map/ppermute | solution.py:19
  54.9 5.0 %collective-permute-start.5 = (f32[1,1,128]{2,1,0:T(1,128)S(1)}, f32[1,1,128]{2,1,0:T(1,128)S(1)}, u32[]{:S(2)}, u32[]{:S(2)}) collective-permute-start(f32[1,1,128]{2,1,0:T(1,128)S(1)} %get-tuple-element.78), channel_id=1, source_target_pairs={{4,0},{8,4},{12,8},{5,1},{9,5},{13,9},{6,2},{10,6},{14,10},{7,3},{... | collective-permute-start | bytes 1544 | tf_op jit(solution)/shard_map/ppermute | solution.py:21
  60.0 7.5 %collective-permute-start.6 = (f32[1,18,1]{2,1,0:T(8,128)S(1)}, f32[1,18,1]{2,1,0:T(8,128)S(1)}, u32[]{:S(2)}, u32[]{:S(2)}) collective-permute-start(f32[1,18,1]{2,1,0:T(8,128)S(1)} %get-tuple-element.67), channel_id=1, source_target_pairs={{0,1},{1,2},{2,3},{3,0},{4,5},{5,6},{6,7},{7,4},{8,9},{9,10},{10,1... | collective-permute-start | bytes 224 | tf_op jit(solution)/shard_map/ppermute | solution.py:19
  60.8 5.8 %collective-permute-start.2 = (f32[2,18,1]{2,1,0:T(8,128)S(1)}, f32[2,18,1]{2,1,0:T(8,128)S(1)}, u32[]{:S(2)}, u32[]{:S(2)}) collective-permute-start(f32[2,18,1]{2,1,0:T(8,128)S(1)} %get-tuple-element.55), channel_id=1, source_target_pairs={{0,1},{1,2},{2,3},{3,0},{4,5},{5,6},{6,7},{7,4},{8,9},{9,10},{10,1... | collective-permute-start | bytes 440 | tf_op jit(solution)/shard_map/ppermute | solution.py:19
  61.0 5.7 %collective-permute-start.3 = (f32[2,18,1]{2,1,0:T(8,128)S(1)}, f32[2,18,1]{2,1,0:T(8,128)S(1)}, u32[]{:S(2)}, u32[]{:S(2)}) collective-permute-start(f32[2,18,1]{2,1,0:T(8,128)S(1)} %get-tuple-element.56), channel_id=1, source_target_pairs={{1,0},{2,1},{3,2},{0,3},{5,4},{6,5},{7,6},{4,7},{9,8},{10,9},{11,1... | collective-permute-start | bytes 440 | tf_op jit(solution)/shard_map/ppermute | solution.py:21
  64.7 3.7 %collective-permute-start.7 = (f32[1,18,1]{2,1,0:T(8,128)S(1)}, f32[1,18,1]{2,1,0:T(8,128)S(1)}, u32[]{:S(2)}, u32[]{:S(2)}) collective-permute-start(f32[1,18,1]{2,1,0:T(8,128)S(1)} %get-tuple-element.68), channel_id=1, source_target_pairs={{1,0},{2,1},{3,2},{0,3},{5,4},{6,5},{7,6},{4,7},{9,8},{10,9},{11,1... | collective-permute-start | bytes 224 | tf_op jit(solution)/shard_map/ppermute | solution.py:21
  69.7 3.9 %collective-permute-start.8 = (f32[1,1,128]{2,1,0:T(1,128)S(1)}, f32[1,1,128]{2,1,0:T(1,128)S(1)}, u32[]{:S(2)}, u32[]{:S(2)}) collective-permute-start(f32[1,1,128]{2,1,0:T(1,128)S(1)} %get-tuple-element.75), channel_id=1, source_target_pairs={{0,4},{4,8},{8,12},{1,5},{5,9},{9,13},{2,6},{6,10},{10,14},{3,7},{... | collective-permute-start | bytes 1544 | tf_op jit(solution)/shard_map/ppermute | solution.py:19
  72.3 6.0 %collective-permute-start.9 = (f32[1,1,128]{2,1,0:T(1,128)S(1)}, f32[1,1,128]{2,1,0:T(1,128)S(1)}, u32[]{:S(2)}, u32[]{:S(2)}) collective-permute-start(f32[1,1,128]{2,1,0:T(1,128)S(1)} %get-tuple-element.76), channel_id=1, source_target_pairs={{4,0},{8,4},{12,8},{5,1},{9,5},{13,9},{6,2},{10,6},{14,10},{7,3},{... | collective-permute-start | bytes 1544 | tf_op jit(solution)/shard_map/ppermute | solution.py:21
  78.4 5.5 %collective-permute-start.10 = (f32[1,18,1]{2,1,0:T(8,128)S(1)}, f32[1,18,1]{2,1,0:T(8,128)S(1)}, u32[]{:S(2)}, u32[]{:S(2)}) collective-permute-start(f32[1,18,1]{2,1,0:T(8,128)S(1)} %get-tuple-element.65), channel_id=1, source_target_pairs={{0,1},{1,2},{2,3},{3,0},{4,5},{5,6},{6,7},{7,4},{8,9},{9,10},{10,1... | collective-permute-start | bytes 224 | tf_op jit(solution)/shard_map/ppermute | solution.py:19
  78.4 5.5 %collective-permute-start.11 = (f32[1,18,1]{2,1,0:T(8,128)S(1)}, f32[1,18,1]{2,1,0:T(8,128)S(1)}, u32[]{:S(2)}, u32[]{:S(2)}) collective-permute-start(f32[1,18,1]{2,1,0:T(8,128)S(1)} %get-tuple-element.66), channel_id=1, source_target_pairs={{1,0},{2,1},{3,2},{0,3},{5,4},{6,5},{7,6},{4,7},{9,8},{10,9},{11,1... | collective-permute-start | bytes 224 | tf_op jit(solution)/shard_map/ppermute | solution.py:21
  85.2 4.6 %collective-permute-start.12 = (f32[1,1,128]{2,1,0:T(1,128)S(1)}, f32[1,1,128]{2,1,0:T(1,128)S(1)}, u32[]{:S(2)}, u32[]{:S(2)}) collective-permute-start(f32[1,1,128]{2,1,0:T(1,128)S(1)} %get-tuple-element.73), channel_id=1, source_target_pairs={{0,4},{4,8},{8,12},{1,5},{5,9},{9,13},{2,6},{6,10},{10,14},{3,7},{... | collective-permute-start | bytes 1544 | tf_op jit(solution)/shard_map/ppermute | solution.py:19
  88.6 3.5 %collective-permute-start.13 = (f32[1,1,128]{2,1,0:T(1,128)S(1)}, f32[1,1,128]{2,1,0:T(1,128)S(1)}, u32[]{:S(2)}, u32[]{:S(2)}) collective-permute-start(f32[1,1,128]{2,1,0:T(1,128)S(1)} %get-tuple-element.74), channel_id=1, source_target_pairs={{4,0},{8,4},{12,8},{5,1},{9,5},{13,9},{6,2},{10,6},{14,10},{7,3},{... | collective-permute-start | bytes 1544 | tf_op jit(solution)/shard_map/ppermute | solution.py:21
  92.2 5.5 %collective-permute-start.14 = (f32[1,18,1]{2,1,0:T(8,128)S(1)}, f32[1,18,1]{2,1,0:T(8,128)S(1)}, u32[]{:S(2)}, u32[]{:S(2)}) collective-permute-start(f32[1,18,1]{2,1,0:T(8,128)S(1)} %get-tuple-element.63), channel_id=1, source_target_pairs={{0,1},{1,2},{2,3},{3,0},{4,5},{5,6},{6,7},{7,4},{8,9},{9,10},{10,1... | collective-permute-start | bytes 224 | tf_op jit(solution)/shard_map/ppermute | solution.py:19
  93.3 4.4 %collective-permute-start.15 = (f32[1,18,1]{2,1,0:T(8,128)S(1)}, f32[1,18,1]{2,1,0:T(8,128)S(1)}, u32[]{:S(2)}, u32[]{:S(2)}) collective-permute-start(f32[1,18,1]{2,1,0:T(8,128)S(1)} %get-tuple-element.64), channel_id=1, source_target_pairs={{1,0},{2,1},{3,2},{0,3},{5,4},{6,5},{7,6},{4,7},{9,8},{10,9},{11,1... | collective-permute-start | bytes 224 | tf_op jit(solution)/shard_map/ppermute | solution.py:21
  99.0 4.7 %collective-permute-start.16 = (f32[1,1,128]{2,1,0:T(1,128)S(1)}, f32[1,1,128]{2,1,0:T(1,128)S(1)}, u32[]{:S(2)}, u32[]{:S(2)}) collective-permute-start(f32[1,1,128]{2,1,0:T(1,128)S(1)} %get-tuple-element.71), channel_id=1, source_target_pairs={{0,4},{4,8},{8,12},{1,5},{5,9},{9,13},{2,6},{6,10},{10,14},{3,7},{... | collective-permute-start | bytes 1544 | tf_op jit(solution)/shard_map/ppermute | solution.py:19
  102.4 3.5 %collective-permute-start.17 = (f32[1,1,128]{2,1,0:T(1,128)S(1)}, f32[1,1,128]{2,1,0:T(1,128)S(1)}, u32[]{:S(2)}, u32[]{:S(2)}) collective-permute-start(f32[1,1,128]{2,1,0:T(1,128)S(1)} %get-tuple-element.72), channel_id=1, source_target_pairs={{4,0},{8,4},{12,8},{5,1},{9,5},{13,9},{6,2},{10,6},{14,10},{7,3},{... | collective-permute-start | bytes 1544 | tf_op jit(solution)/shard_map/ppermute | solution.py:21
  106.0 5.5 %collective-permute-start.18 = (f32[1,18,1]{2,1,0:T(8,128)S(1)}, f32[1,18,1]{2,1,0:T(8,128)S(1)}, u32[]{:S(2)}, u32[]{:S(2)}) collective-permute-start(f32[1,18,1]{2,1,0:T(8,128)S(1)} %get-tuple-element.61), channel_id=1, source_target_pairs={{0,1},{1,2},{2,3},{3,0},{4,5},{5,6},{6,7},{7,4},{8,9},{9,10},{10,1... | collective-permute-start | bytes 224 | tf_op jit(solution)/shard_map/ppermute | solution.py:19
  107.3 4.2 %collective-permute-start.19 = (f32[1,18,1]{2,1,0:T(8,128)S(1)}, f32[1,18,1]{2,1,0:T(8,128)S(1)}, u32[]{:S(2)}, u32[]{:S(2)}) collective-permute-start(f32[1,18,1]{2,1,0:T(8,128)S(1)} %get-tuple-element.62), channel_id=1, source_target_pairs={{1,0},{2,1},{3,2},{0,3},{5,4},{6,5},{7,6},{4,7},{9,8},{10,9},{11,1... | collective-permute-start | bytes 224 | tf_op jit(solution)/shard_map/ppermute | solution.py:21
  112.8 9.5 %collective-permute-start.20 = (f32[1,1,128]{2,1,0:T(1,128)S(1)}, f32[1,1,128]{2,1,0:T(1,128)S(1)}, u32[]{:S(2)}, u32[]{:S(2)}) collective-permute-start(f32[1,1,128]{2,1,0:T(1,128)S(1)} %get-tuple-element.69), channel_id=1, source_target_pairs={{0,4},{4,8},{8,12},{1,5},{5,9},{9,13},{2,6},{6,10},{10,14},{3,7},{... | collective-permute-start | bytes 1544 | tf_op jit(solution)/shard_map/ppermute | solution.py:19
  116.2 6.1 %collective-permute-start.21 = (f32[1,1,128]{2,1,0:T(1,128)S(1)}, f32[1,1,128]{2,1,0:T(1,128)S(1)}, u32[]{:S(2)}, u32[]{:S(2)}) collective-permute-start(f32[1,1,128]{2,1,0:T(1,128)S(1)} %get-tuple-element.70), channel_id=1, source_target_pairs={{4,0},{8,4},{12,8},{5,1},{9,5},{13,9},{6,2},{10,6},{14,10},{7,3},{... | collective-permute-start | bytes 1544 | tf_op jit(solution)/shard_map/ppermute | solution.py:21
  117.5 14.9 %collective-permute-start.24 = (bf16[1,1,128,128]{3,2,1,0:T(8,128)(2,1)S(1)}, bf16[1,1,128,128]{3,2,1,0:T(8,128)(2,1)S(1)}, u32[]{:S(2)}, u32[]{:S(2)}) collective-permute-start(bf16[1,1,128,128]{3,2,1,0:T(8,128)(2,1)S(1)} %get-tuple-element.52), channel_id=1, source_target_pairs={{0,4},{4,8},{8,12},{1,5},{5,9},{9,13},{2,6},{6,10},{10,14},{3,7},{... | collective-permute-start | bytes 98312 | tf_op jit(solution)/shard_map/ppermute | solution.py:19
  121.0 11.5 %collective-permute-start.25 = (bf16[1,1,128,128]{3,2,1,0:T(8,128)(2,1)S(1)}, bf16[1,1,128,128]{3,2,1,0:T(8,128)(2,1)S(1)}, u32[]{:S(2)}, u32[]{:S(2)}) collective-permute-start(bf16[1,1,128,128]{3,2,1,0:T(8,128)(2,1)S(1)} %get-tuple-element.51), channel_id=1, source_target_pairs={{4,0},{8,4},{12,8},{5,1},{9,5},{13,9},{6,2},{10,6},{14,10},{7,3},{... | collective-permute-start | bytes 98312 | tf_op jit(solution)/shard_map/ppermute | solution.py:21
  122.4 5.5 %collective-permute-start.22 = (f32[1,18,1]{2,1,0:T(8,128)S(1)}, f32[1,18,1]{2,1,0:T(8,128)S(1)}, u32[]{:S(2)}, u32[]{:S(2)}) collective-permute-start(f32[1,18,1]{2,1,0:T(8,128)S(1)} %get-tuple-element.59), channel_id=1, source_target_pairs={{0,1},{1,2},{2,3},{3,0},{4,5},{5,6},{6,7},{7,4},{8,9},{9,10},{10,1... | collective-permute-start | bytes 224 | tf_op jit(solution)/shard_map/ppermute | solution.py:19
  123.7 4.2 %collective-permute-start.23 = (f32[1,18,1]{2,1,0:T(8,128)S(1)}, f32[1,18,1]{2,1,0:T(8,128)S(1)}, u32[]{:S(2)}, u32[]{:S(2)}) collective-permute-start(f32[1,18,1]{2,1,0:T(8,128)S(1)} %get-tuple-element.60), channel_id=1, source_target_pairs={{1,0},{2,1},{3,2},{0,3},{5,4},{6,5},{7,6},{4,7},{9,8},{10,9},{11,1... | collective-permute-start | bytes 224 | tf_op jit(solution)/shard_map/ppermute | solution.py:21
  132.5 4.4 %copy-start.1 = (bf16[3,3,128,128]{3,2,1,0:T(8,128)(2,1)S(1)}, bf16[3,3,128,128]{3,2,1,0:T(8,128)(2,1)}, u32[]{:S(2)}) copy-start(bf16[3,3,128,128]{3,2,1,0:T(8,128)(2,1)} %param.10) | copy-start | bytes 884740
  132.9 5.6 %collective-permute-start.26 = (bf16[1,18,1,128]{3,2,1,0:T(2,128)(2,1)S(1)}, bf16[1,18,1,128]{3,2,1,0:T(2,128)(2,1)S(1)}, u32[]{:S(2)}, u32[]{:S(2)}) collective-permute-start(bf16[1,18,1,128]{3,2,1,0:T(2,128)(2,1)S(1)} %get-tuple-element.42), channel_id=1, source_target_pairs={{0,1},{1,2},{2,3},{3,0},{4,5},{5,6},{6,7},{7,4},{8,9},{9,10},{10,1... | collective-permute-start | bytes 13832 | tf_op jit(solution)/shard_map/ppermute | solution.py:19
  134.2 4.2 %collective-permute-start.27 = (bf16[1,18,1,128]{3,2,1,0:T(2,128)(2,1)S(1)}, bf16[1,18,1,128]{3,2,1,0:T(2,128)(2,1)S(1)}, u32[]{:S(2)}, u32[]{:S(2)}) collective-permute-start(bf16[1,18,1,128]{3,2,1,0:T(2,128)(2,1)S(1)} %get-tuple-element.43), channel_id=1, source_target_pairs={{1,0},{2,1},{3,2},{0,3},{5,4},{6,5},{7,6},{4,7},{9,8},{10,9},{11,1... | collective-permute-start | bytes 13832 | tf_op jit(solution)/shard_map/ppermute | solution.py:21
  139.6 0.7 copy-start.4
  141.4 0.7 copy-start.5
  146.0 0.8 copy-start.2
  146.9 49.1 %collective-permute-start.28 = (bf16[1,1,128,128]{3,2,1,0:T(8,128)(2,1)S(1)}, bf16[1,1,128,128]{3,2,1,0:T(8,128)(2,1)S(1)}, u32[]{:S(2)}, u32[]{:S(2)}) collective-permute-start(bf16[1,1,128,128]{3,2,1,0:T(8,128)(2,1)S(1)} %get-tuple-element.46), channel_id=1, source_target_pairs={{0,4},{4,8},{8,12},{1,5},{5,9},{9,13},{2,6},{6,10},{10,14},{3,7},{... | collective-permute-start | bytes 98312 | tf_op jit(solution)/shard_map/ppermute | solution.py:19
  149.1 46.9 %collective-permute-start.29 = (bf16[1,1,128,128]{3,2,1,0:T(8,128)(2,1)S(1)}, bf16[1,1,128,128]{3,2,1,0:T(8,128)(2,1)S(1)}, u32[]{:S(2)}, u32[]{:S(2)}) collective-permute-start(bf16[1,1,128,128]{3,2,1,0:T(8,128)(2,1)S(1)} %get-tuple-element.47), channel_id=1, source_target_pairs={{4,0},{8,4},{12,8},{5,1},{9,5},{13,9},{6,2},{10,6},{14,10},{7,3},{... | collective-permute-start | bytes 98312 | tf_op jit(solution)/shard_map/ppermute | solution.py:21
  196.0 3.7 %collective-permute-start.30 = (bf16[1,18,1,128]{3,2,1,0:T(2,128)(2,1)S(1)}, bf16[1,18,1,128]{3,2,1,0:T(2,128)(2,1)S(1)}, u32[]{:S(2)}, u32[]{:S(2)}) collective-permute-start(bf16[1,18,1,128]{3,2,1,0:T(2,128)(2,1)S(1)} %get-tuple-element.37), channel_id=1, source_target_pairs={{1,0},{2,1},{3,2},{0,3},{5,4},{6,5},{7,6},{4,7},{9,8},{10,9},{11,1... | collective-permute-start | bytes 13832 | tf_op jit(solution)/shard_map/ppermute | solution.py:21
  198.3 5.5 %collective-permute-start.31 = (bf16[1,18,1,128]{3,2,1,0:T(2,128)(2,1)S(1)}, bf16[1,18,1,128]{3,2,1,0:T(2,128)(2,1)S(1)}, u32[]{:S(2)}, u32[]{:S(2)}) collective-permute-start(bf16[1,18,1,128]{3,2,1,0:T(2,128)(2,1)S(1)} %get-tuple-element.38), channel_id=1, source_target_pairs={{0,1},{1,2},{2,3},{3,0},{4,5},{5,6},{6,7},{7,4},{8,9},{9,10},{10,1... | collective-permute-start | bytes 13832 | tf_op jit(solution)/shard_map/ppermute | solution.py:19
Sparse Core Ops, SparseCore 0:
  147.0 57.9 reduce-scatter.1
where the time goes:
time: 227 us; the launch traced here: 225 us
  blocking collectives  91.5 us (40%)
  starting transfers between devices  60.1 us (26%)
  waiting for transfers between devices  23.7 us (10%)
  other arithmetic  18.9 us (8%)
  between operations  15.9 us (7%)
  matrix products  9.55 us (4%)
  local copies, waits for them, and re-layouts  5.66 us (2%)
    psum x1, blocking collectives, shards(): lax.psum((local_bias, local_proj), ('dp', 'lat', 'lon'))  45 us
    psum x1, blocking collectives, shards(): lax.psum((jnp.sum(mask_float), jnp.sum(mask_float * surface_cotangent, ax...  36.6 us
    ppermute x16, starting transfers between devices, extended(): lax.ppermute(head, axis, [((i + 1) % count, i) for i in range(ends)])  32.9 us
    ppermute x16, starting transfers between devices, extended(): lax.ppermute(tail, axis, [(i, (i + 1) % count) for i in range(ends)])  27.1 us
    ppermute x16, waiting for transfers between devices, extended(): lax.ppermute(tail, axis, [(i, (i + 1) % count) for i in range(ends)])  11.9 us
    ppermute x16, waiting for transfers between devices, extended(): lax.ppermute(head, axis, [((i + 1) % count, i) for i in range(ends)])  11.7 us
    psum x1, blocking collectives, shards(): own_weight = lax.psum(spatial, 'dp')  9.87 us
    add x4, other arithmetic, solve_steps(): direction = residual + step_beta[turn_index] * direction  5.32 us
  transfers between devices with their start and end apart: 33, of which 12 were waited for; matrix products, arithmetic and copies ran while one was open for 8% of the time, Pallas kernels for 0%

commit v1 on v0

--- a/solution.py
+++ b/solution.py
@@ -73,7 +73,10 @@
     samples, lat_rows, lon_cols, channels = hidden_in.shape
     mask_float = sea_mask.astype(jnp.float32)
     counted, summed = lax.psum(
-        (jnp.sum(mask_float), jnp.sum(mask_float * surface_cotangent, axis=(1, 2))), ("lat", "lon")
+        lax.psum(
+            (jnp.sum(mask_float), jnp.sum(mask_float * surface_cotangent, axis=(1, 2))), "lon"
+        ),
+        "lat",
     )
     adjoint_start = mask_float * (surface_cotangent - (summed / counted)[:, None, None])
     coefs = jnp.stack([mask_float, ocean_depth])

time: 227 us -> 212 us (0.934)
  blocking collectives: 91.5 us -> 76.5 us
    psum x1, blocking collectives: 36.6 us -> 13.4 us  [shards(): lax.psum((jnp.sum(mask_float), jnp.sum(mask_float * surface_cotangent, ax...]
    psum x0 -> x1, blocking collectives: none -> 8.21 us  [shards(): lax.psum(lax.psum((jnp.sum(mask_float), jnp.sum(mask_float * surface_cota...]
where the time goes in v1:
time: 212 us; the launch traced here: 211 us
  blocking collectives  76.5 us (36%)
  starting transfers between devices  61 us (29%)
  waiting for transfers between devices  23.2 us (11%)
  other arithmetic  18.8 us (9%)
  between operations  15.9 us (8%)
  matrix products  9.56 us (5%)
  local copies, waits for them, and re-layouts  5.63 us (3%)
    psum x1, blocking collectives, shards(): lax.psum((local_bias, local_proj), ('dp', 'lat', 'lon'))  45 us
    ppermute x16, starting transfers between devices, extended(): lax.ppermute(head, axis, [((i + 1) % count, i) for i in range(ends)])  32.8 us
    ppermute x16, starting transfers between devices, extended(): lax.ppermute(tail, axis, [(i, (i + 1) % count) for i in range(ends)])  28.1 us
    psum x1, blocking collectives, shards(): lax.psum((jnp.sum(mask_float), jnp.sum(mask_float * surface_cotangent, ax...  13.4 us
    ppermute x16, waiting for transfers between devices, extended(): lax.ppermute(tail, axis, [(i, (i + 1) % count) for i in range(ends)])  11.9 us
    ppermute x16, waiting for transfers between devices, extended(): lax.ppermute(head, axis, [((i + 1) % count, i) for i in range(ends)])  11.3 us
    psum x1, blocking collectives, shards(): own_weight = lax.psum(spatial, 'dp')  9.88 us
    psum x1, blocking collectives, shards(): lax.psum(lax.psum((jnp.sum(mask_float), jnp.sum(mask_float * surface_cota...  8.21 us
  transfers between devices with their start and end apart: 33, of which 12 were waited for; matrix products, arithmetic and copies ran while one was open for 8% of the time, Pallas kernels for 0%

profile of v1, /device:TPU:0, one launch (start us, length us, event | category | flops | bytes accessed | tf_op | source)
XLA Modules:
  0.0 210.6 jit_solution(14255143070344174793)
XLA Ops:
  8.7 2.4 %collective-permute-start = (f32[2,1,128]{2,1,0:T(1,128)S(1)}, f32[2,1,128]{2,1,0:T(1,128)S(1)}, u32[]{:S(2)}, u32[]{:S(2)}) collective-permute-start(f32[2,1,128]{2,1,0:T(1,128)S(1)} %get-tuple-element.59), channel_id=1, source_target_pairs={{0,4},{4,8},{8,12},{1,5},{5,9},{9,13},{2,6},{6,10},{10,14},{3,7},{... | collective-permute-start | bytes 3080 | tf_op jit(solution)/shard_map/ppermute | solution.py:19
  11.1 1.3 collective-permute-start.1
  12.4 1.3 convert_reduce_fusion.1
  13.7 1.3 multiply_reduce_fusion.1
  15.0 13.4 %all-reduce.1 = (f32[1]{0:T(128)}, f32[]{:T(128)}) all-reduce(f32[1]{0:T(128)} %bitcast.2, f32[]{:T(128)} %convert_reduce_fusion.1), channel_id=1, replica_groups=mesh['dp'=2,'lat'=4,'lon'=4] {'lon'}, use_global_device_ids=true, to_apply=%region_1.0 | all-reduce | flops 2 | bytes 16 | tf_op jit(solution)/shard_map/psum | solution.py:76
  28.4 8.2 %all-reduce.2 = (f32[1]{0:T(128)}, f32[1]{0:T(128)}) all-reduce(f32[1]{0:T(128)} %get-tuple-element.6, f32[1]{0:T(128)} %bitcast.3), channel_id=1, replica_groups=mesh['dp'=2,'lat'=4,'lon'=4] {'lat'}, use_global_device_ids=true, to_apply=%region_2.0 | all-reduce | flops 2 | bytes 16 | tf_op jit(solution)/shard_map/psum | solution.py:75
  38.7 2.2 %collective-permute-start.4 = (f32[1,1,128]{2,1,0:T(1,128)S(1)}, f32[1,1,128]{2,1,0:T(1,128)S(1)}, u32[]{:S(2)}, u32[]{:S(2)}) collective-permute-start(f32[1,1,128]{2,1,0:T(1,128)S(1)} %get-tuple-element.79), channel_id=1, source_target_pairs={{0,4},{4,8},{8,12},{1,5},{5,9},{9,13},{2,6},{6,10},{10,14},{3,7},{... | collective-permute-start | bytes 1544 | tf_op jit(solution)/shard_map/ppermute | solution.py:19
  40.9 1.3 collective-permute-start.5
  42.2 1.5 fusion.171
  43.8 1.4 fusion.172
  46.5 3.7 %collective-permute-start.3 = (f32[2,18,1]{2,1,0:T(8,128)S(1)}, f32[2,18,1]{2,1,0:T(8,128)S(1)}, u32[]{:S(2)}, u32[]{:S(2)}) collective-permute-start(f32[2,18,1]{2,1,0:T(8,128)S(1)} %get-tuple-element.58), channel_id=1, source_target_pairs={{1,0},{2,1},{3,2},{0,3},{5,4},{6,5},{7,6},{4,7},{9,8},{10,9},{11,1... | collective-permute-start | bytes 440 | tf_op jit(solution)/shard_map/ppermute | solution.py:21
  50.2 2.0 collective-permute-start.7
  53.9 1.4 multiply_add_fusion.3
  55.3 2.5 %collective-permute-start.8 = (f32[1,1,128]{2,1,0:T(1,128)S(1)}, f32[1,1,128]{2,1,0:T(1,128)S(1)}, u32[]{:S(2)}, u32[]{:S(2)}) collective-permute-start(f32[1,1,128]{2,1,0:T(1,128)S(1)} %get-tuple-element.77), channel_id=1, source_target_pairs={{0,4},{4,8},{8,12},{1,5},{5,9},{9,13},{2,6},{6,10},{10,14},{3,7},{... | collective-permute-start | bytes 1544 | tf_op jit(solution)/shard_map/ppermute | solution.py:19
  57.9 1.3 collective-permute-start.9
  59.2 4.7 %collective-permute-done.9 = f32[1,1,128]{2,1,0:T(1,128)S(1)} collective-permute-done((f32[1,1,128]{2,1,0:T(1,128)S(1)}, f32[1,1,128]{2,1,0:T(1,128)S(1)}, u32[]{:S(2)}, u32[]{:S(2)}) %collective-permute-start.9) | collective-permute-done | bytes 544 | tf_op jit(solution)/shard_map/ppermute | solution.py:21
  64.0 3.8 %collective-permute-start.11 = (f32[1,18,1]{2,1,0:T(8,128)S(1)}, f32[1,18,1]{2,1,0:T(8,128)S(1)}, u32[]{:S(2)}, u32[]{:S(2)}) collective-permute-start(f32[1,18,1]{2,1,0:T(8,128)S(1)} %get-tuple-element.68), channel_id=1, source_target_pairs={{1,0},{2,1},{3,2},{0,3},{5,4},{6,5},{7,6},{4,7},{9,8},{10,9},{11,1... | collective-permute-start | bytes 224 | tf_op jit(solution)/shard_map/ppermute | solution.py:21
  67.8 1.7 collective-permute-done.10
  69.4 1.4 multiply_add_fusion.2
  70.8 3.3 %collective-permute-start.12 = (f32[1,1,128]{2,1,0:T(1,128)S(1)}, f32[1,1,128]{2,1,0:T(1,128)S(1)}, u32[]{:S(2)}, u32[]{:S(2)}) collective-permute-start(f32[1,1,128]{2,1,0:T(1,128)S(1)} %get-tuple-element.75), channel_id=1, source_target_pairs={{0,4},{4,8},{8,12},{1,5},{5,9},{9,13},{2,6},{6,10},{10,14},{3,7},{... | collective-permute-start | bytes 1544 | tf_op jit(solution)/shard_map/ppermute | solution.py:19
  74.1 1.3 collective-permute-start.13
  75.4 2.2 %collective-permute-done.13 = f32[1,1,128]{2,1,0:T(1,128)S(1)} collective-permute-done((f32[1,1,128]{2,1,0:T(1,128)S(1)}, f32[1,1,128]{2,1,0:T(1,128)S(1)}, u32[]{:S(2)}, u32[]{:S(2)}) %collective-permute-start.13) | collective-permute-done | bytes 544 | tf_op jit(solution)/shard_map/ppermute | solution.py:21
  78.8 2.8 %collective-permute-start.15 = (f32[1,18,1]{2,1,0:T(8,128)S(1)}, f32[1,18,1]{2,1,0:T(8,128)S(1)}, u32[]{:S(2)}, u32[]{:S(2)}) collective-permute-start(f32[1,18,1]{2,1,0:T(8,128)S(1)} %get-tuple-element.66), channel_id=1, source_target_pairs={{1,0},{2,1},{3,2},{0,3},{5,4},{6,5},{7,6},{4,7},{9,8},{10,9},{11,1... | collective-permute-start | bytes 224 | tf_op jit(solution)/shard_map/ppermute | solution.py:21
  81.6 1.6 collective-permute-done.14
  83.2 1.4 multiply_add_fusion.1
  84.6 3.4 %collective-permute-start.16 = (f32[1,1,128]{2,1,0:T(1,128)S(1)}, f32[1,1,128]{2,1,0:T(1,128)S(1)}, u32[]{:S(2)}, u32[]{:S(2)}) collective-permute-start(f32[1,1,128]{2,1,0:T(1,128)S(1)} %get-tuple-element.73), channel_id=1, source_target_pairs={{0,4},{4,8},{8,12},{1,5},{5,9},{9,13},{2,6},{6,10},{10,14},{3,7},{... | collective-permute-start | bytes 1544 | tf_op jit(solution)/shard_map/ppermute | solution.py:19
  88.0 1.3 collective-permute-start.17
  89.3 2.2 %collective-permute-done.17 = f32[1,1,128]{2,1,0:T(1,128)S(1)} collective-permute-done((f32[1,1,128]{2,1,0:T(1,128)S(1)}, f32[1,1,128]{2,1,0:T(1,128)S(1)}, u32[]{:S(2)}, u32[]{:S(2)}) %collective-permute-start.17) | collective-permute-done | bytes 544 | tf_op jit(solution)/shard_map/ppermute | solution.py:21
  91.5 1.3 collective-permute-start.18
  92.8 2.6 %collective-permute-start.19 = (f32[1,18,1]{2,1,0:T(8,128)S(1)}, f32[1,18,1]{2,1,0:T(8,128)S(1)}, u32[]{:S(2)}, u32[]{:S(2)}) collective-permute-start(f32[1,18,1]{2,1,0:T(8,128)S(1)} %get-tuple-element.64), channel_id=1, source_target_pairs={{1,0},{2,1},{3,2},{0,3},{5,4},{6,5},{7,6},{4,7},{9,8},{10,9},{11,1... | collective-permute-start | bytes 224 | tf_op jit(solution)/shard_map/ppermute | solution.py:21
  95.5 1.6 collective-permute-done.18
  98.3 3.4 %collective-permute-start.20 = (f32[1,1,128]{2,1,0:T(1,128)S(1)}, f32[1,1,128]{2,1,0:T(1,128)S(1)}, u32[]{:S(2)}, u32[]{:S(2)}) collective-permute-start(f32[1,1,128]{2,1,0:T(1,128)S(1)} %get-tuple-element.71), channel_id=1, source_target_pairs={{0,4},{4,8},{8,12},{1,5},{5,9},{9,13},{2,6},{6,10},{10,14},{3,7},{... | collective-permute-start | bytes 1544 | tf_op jit(solution)/shard_map/ppermute | solution.py:19
  101.7 1.3 collective-permute-start.21
  103.0 3.5 %collective-permute-start.24 = (bf16[1,1,128,128]{3,2,1,0:T(8,128)(2,1)S(1)}, bf16[1,1,128,128]{3,2,1,0:T(8,128)(2,1)S(1)}, u32[]{:S(2)}, u32[]{:S(2)}) collective-permute-start(bf16[1,1,128,128]{3,2,1,0:T(8,128)(2,1)S(1)} %get-tuple-element.54), channel_id=1, source_target_pairs={{0,4},{4,8},{8,12},{1,5},{5,9},{9,13},{2,6},{6,10},{10,14},{3,7},{... | collective-permute-start | bytes 98312 | tf_op jit(solution)/shard_map/ppermute | solution.py:19
  106.4 1.3 collective-permute-start.25
  107.9 1.3 collective-permute-start.22
  109.2 2.6 %collective-permute-start.23 = (f32[1,18,1]{2,1,0:T(8,128)S(1)}, f32[1,18,1]{2,1,0:T(8,128)S(1)}, u32[]{:S(2)}, u32[]{:S(2)}) collective-permute-start(f32[1,18,1]{2,1,0:T(8,128)S(1)} %get-tuple-element.62), channel_id=1, source_target_pairs={{1,0},{2,1},{3,2},{0,3},{5,4},{6,5},{7,6},{4,7},{9,8},{10,9},{11,1... | collective-permute-start | bytes 224 | tf_op jit(solution)/shard_map/ppermute | solution.py:21
  111.8 1.6 collective-permute-done.22
  113.4 4.4 %fusion.69 = f32[2048]{0:T(1024)S(1)} fusion(f32[1,16,128]{2,1,0:T(8,128)S(1)} %get-tuple-element.13, f32[1,16,128]{2,1,0:T(8,128)S(1)} %get-tuple-element.23, f32[1,16,128]{2,1,0:T(8,128)S(1)} %get-tuple-element.12, f32[1,18,1]{2,1,0:T(8,128)S(1)} %collective-permute-done.23, f32[1,1,128]{2,1,0:T(1,128)S(1)} %collective-permute-done.21, ...), kind=kLoop, calls=%fused_computation.128 | loop fusion | flops 79872 | bytes 107692 | tf_op jit(solution)/shard_map/mul | solution.py:108
  118.2 1.4 collective-permute-start.26
  119.6 2.6 %collective-permute-start.27 = (bf16[1,18,1,128]{3,2,1,0:T(2,128)(2,1)S(1)}, bf16[1,18,1,128]{3,2,1,0:T(2,128)(2,1)S(1)}, u32[]{:S(2)}, u32[]{:S(2)}) collective-permute-start(bf16[1,18,1,128]{3,2,1,0:T(2,128)(2,1)S(1)} %get-tuple-element.45), channel_id=1, source_target_pairs={{1,0},{2,1},{3,2},{0,3},{5,4},{6,5},{7,6},{4,7},{9,8},{10,9},{11,1... | collective-permute-start | bytes 13832 | tf_op jit(solution)/shard_map/ppermute | solution.py:21
  122.5 1.3 collective-permute-done.26
  132.3 2.2 %collective-permute-start.28 = (bf16[1,1,128,128]{3,2,1,0:T(8,128)(2,1)S(1)}, bf16[1,1,128,128]{3,2,1,0:T(8,128)(2,1)S(1)}, u32[]{:S(2)}, u32[]{:S(2)}) collective-permute-start(bf16[1,1,128,128]{3,2,1,0:T(8,128)(2,1)S(1)} %get-tuple-element.48), channel_id=1, source_target_pairs={{0,4},{4,8},{8,12},{1,5},{5,9},{9,13},{2,6},{6,10},{10,14},{3,7},{... | collective-permute-start | bytes 98312 | tf_op jit(solution)/shard_map/ppermute | solution.py:19
  134.5 1.3 collective-permute-start.29
  135.8 45.0 %all-reduce = (f32[128]{0:T(128)S(1)}, f32[128]{0:T(128)S(1)}) all-reduce(f32[128]{0:T(128)S(1)} %get-tuple-element.10, f32[128]{0:T(128)S(1)} %get-tuple-element.24), channel_id=1, replica_groups=mesh['dp'=2,'lat'=4,'lon'=4] {'dp','lat','lon'}, use_global_device_ids=true, to_apply=%region_9.0 | all-reduce | flops 256 | bytes 2048 | tf_op jit(solution)/shard_map/psum | solution.py:143
  181.4 2.3 %collective-permute-start.30 = (bf16[1,18,1,128]{3,2,1,0:T(2,128)(2,1)S(1)}, bf16[1,18,1,128]{3,2,1,0:T(2,128)(2,1)S(1)}, u32[]{:S(2)}, u32[]{:S(2)}) collective-permute-start(bf16[1,18,1,128]{3,2,1,0:T(2,128)(2,1)S(1)} %get-tuple-element.39), channel_id=1, source_target_pairs={{1,0},{2,1},{3,2},{0,3},{5,4},{6,5},{7,6},{4,7},{9,8},{10,9},{11,1... | collective-permute-start | bytes 13832 | tf_op jit(solution)/shard_map/ppermute | solution.py:21
  185.1 4.1 %collective-permute-done.31 = bf16[1,18,1,128]{3,2,1,0:T(2,128)(2,1)S(1)} collective-permute-done((bf16[1,18,1,128]{3,2,1,0:T(2,128)(2,1)S(1)}, bf16[1,18,1,128]{3,2,1,0:T(2,128)(2,1)S(1)}, u32[]{:S(2)}, u32[]{:S(2)}) %collective-permute-start.31) | collective-permute-done | bytes 4640 | tf_op jit(solution)/shard_map/ppermute | solution.py:19
  193.3 9.9 %psum.53 = f32[8,3,3,128]{3,0,2,1:T(8,128)S(1)} all-reduce(f32[8,3,3,128]{3,0,2,1:T(8,128)} %reduce-scatter.2.cloned.1.call-done), channel_id=1, replica_groups=mesh['dp'=2,'lat'=4,'lon'=4] {'dp'}, use_global_device_ids=true, to_apply=%region_7.0 | all-reduce | flops 9216 | bytes 73728 | tf_op jit(solution)/shard_map/psum | solution.py:142
  (106 shorter events, 23.4 us)
Async XLA Ops:
  7.2 106.2 %copy-start.3 = (s32[16,128]{1,0:T(8,128)S(1)}, s32[16,128]{1,0:T(8,128)}, u32[]{:S(2)}) copy-start(s32[16,128]{1,0:T(8,128)} %param.14) | copy-start | bytes 24580
  7.2 95.8 %copy-start = (bf16[1,16,128,128]{3,2,1,0:T(8,128)(2,1)S(1)}, bf16[1,16,128,128]{3,2,1,0:T(8,128)(2,1)}, u32[]{:S(2)}) copy-start(bf16[1,16,128,128]{3,2,1,0:T(8,128)(2,1)} %param.9) | copy-start | bytes 1572868
  7.2 186.1 %reduce-scatter.2.cloned.1.call-start = ((), (), s32[]{:S(2)}) async-start(), calls=%async_computation.1 | async-start | bytes 626688 | tf_op jit(solution)/shard_map/reduce_scatter | solution.py:136
  8.7 36.9 %collective-permute-start = (f32[2,1,128]{2,1,0:T(1,128)S(1)}, f32[2,1,128]{2,1,0:T(1,128)S(1)}, u32[]{:S(2)}, u32[]{:S(2)}) collective-permute-start(f32[2,1,128]{2,1,0:T(1,128)S(1)} %get-tuple-element.59), channel_id=1, source_target_pairs={{0,4},{4,8},{8,12},{1,5},{5,9},{9,13},{2,6},{6,10},{10,14},{3,7},{... | collective-permute-start | bytes 3080 | tf_op jit(solution)/shard_map/ppermute | solution.py:19
  11.1 34.5 %collective-permute-start.1 = (f32[2,1,128]{2,1,0:T(1,128)S(1)}, f32[2,1,128]{2,1,0:T(1,128)S(1)}, u32[]{:S(2)}, u32[]{:S(2)}) collective-permute-start(f32[2,1,128]{2,1,0:T(1,128)S(1)} %get-tuple-element.60), channel_id=1, source_target_pairs={{4,0},{8,4},{12,8},{5,1},{9,5},{13,9},{6,2},{10,6},{14,10},{7,3},{... | collective-permute-start | bytes 3080 | tf_op jit(solution)/shard_map/ppermute | solution.py:21
  38.7 6.5 %collective-permute-start.4 = (f32[1,1,128]{2,1,0:T(1,128)S(1)}, f32[1,1,128]{2,1,0:T(1,128)S(1)}, u32[]{:S(2)}, u32[]{:S(2)}) collective-permute-start(f32[1,1,128]{2,1,0:T(1,128)S(1)} %get-tuple-element.79), channel_id=1, source_target_pairs={{0,4},{4,8},{8,12},{1,5},{5,9},{9,13},{2,6},{6,10},{10,14},{3,7},{... | collective-permute-start | bytes 1544 | tf_op jit(solution)/shard_map/ppermute | solution.py:19
  40.9 4.5 %collective-permute-start.5 = (f32[1,1,128]{2,1,0:T(1,128)S(1)}, f32[1,1,128]{2,1,0:T(1,128)S(1)}, u32[]{:S(2)}, u32[]{:S(2)}) collective-permute-start(f32[1,1,128]{2,1,0:T(1,128)S(1)} %get-tuple-element.80), channel_id=1, source_target_pairs={{4,0},{8,4},{12,8},{5,1},{9,5},{13,9},{6,2},{10,6},{14,10},{7,3},{... | collective-permute-start | bytes 1544 | tf_op jit(solution)/shard_map/ppermute | solution.py:21
  45.5 7.5 %collective-permute-start.6 = (f32[1,18,1]{2,1,0:T(8,128)S(1)}, f32[1,18,1]{2,1,0:T(8,128)S(1)}, u32[]{:S(2)}, u32[]{:S(2)}) collective-permute-start(f32[1,18,1]{2,1,0:T(8,128)S(1)} %get-tuple-element.69), channel_id=1, source_target_pairs={{0,1},{1,2},{2,3},{3,0},{4,5},{5,6},{6,7},{7,4},{8,9},{9,10},{10,1... | collective-permute-start | bytes 224 | tf_op jit(solution)/shard_map/ppermute | solution.py:19
  46.4 5.8 %collective-permute-start.2 = (f32[2,18,1]{2,1,0:T(8,128)S(1)}, f32[2,18,1]{2,1,0:T(8,128)S(1)}, u32[]{:S(2)}, u32[]{:S(2)}) collective-permute-start(f32[2,18,1]{2,1,0:T(8,128)S(1)} %get-tuple-element.57), channel_id=1, source_target_pairs={{0,1},{1,2},{2,3},{3,0},{4,5},{5,6},{6,7},{7,4},{8,9},{9,10},{10,1... | collective-permute-start | bytes 440 | tf_op jit(solution)/shard_map/ppermute | solution.py:19
  46.5 5.7 %collective-permute-start.3 = (f32[2,18,1]{2,1,0:T(8,128)S(1)}, f32[2,18,1]{2,1,0:T(8,128)S(1)}, u32[]{:S(2)}, u32[]{:S(2)}) collective-permute-start(f32[2,18,1]{2,1,0:T(8,128)S(1)} %get-tuple-element.58), channel_id=1, source_target_pairs={{1,0},{2,1},{3,2},{0,3},{5,4},{6,5},{7,6},{4,7},{9,8},{10,9},{11,1... | collective-permute-start | bytes 440 | tf_op jit(solution)/shard_map/ppermute | solution.py:21
  50.2 3.7 %collective-permute-start.7 = (f32[1,18,1]{2,1,0:T(8,128)S(1)}, f32[1,18,1]{2,1,0:T(8,128)S(1)}, u32[]{:S(2)}, u32[]{:S(2)}) collective-permute-start(f32[1,18,1]{2,1,0:T(8,128)S(1)} %get-tuple-element.70), channel_id=1, source_target_pairs={{1,0},{2,1},{3,2},{0,3},{5,4},{6,5},{7,6},{4,7},{9,8},{10,9},{11,1... | collective-permute-start | bytes 224 | tf_op jit(solution)/shard_map/ppermute | solution.py:21
  55.3 3.9 %collective-permute-start.8 = (f32[1,1,128]{2,1,0:T(1,128)S(1)}, f32[1,1,128]{2,1,0:T(1,128)S(1)}, u32[]{:S(2)}, u32[]{:S(2)}) collective-permute-start(f32[1,1,128]{2,1,0:T(1,128)S(1)} %get-tuple-element.77), channel_id=1, source_target_pairs={{0,4},{4,8},{8,12},{1,5},{5,9},{9,13},{2,6},{6,10},{10,14},{3,7},{... | collective-permute-start | bytes 1544 | tf_op jit(solution)/shard_map/ppermute | solution.py:19
  57.9 6.0 %collective-permute-start.9 = (f32[1,1,128]{2,1,0:T(1,128)S(1)}, f32[1,1,128]{2,1,0:T(1,128)S(1)}, u32[]{:S(2)}, u32[]{:S(2)}) collective-permute-start(f32[1,1,128]{2,1,0:T(1,128)S(1)} %get-tuple-element.78), channel_id=1, source_target_pairs={{4,0},{8,4},{12,8},{5,1},{9,5},{13,9},{6,2},{10,6},{14,10},{7,3},{... | collective-permute-start | bytes 1544 | tf_op jit(solution)/shard_map/ppermute | solution.py:21
  63.9 5.5 %collective-permute-start.10 = (f32[1,18,1]{2,1,0:T(8,128)S(1)}, f32[1,18,1]{2,1,0:T(8,128)S(1)}, u32[]{:S(2)}, u32[]{:S(2)}) collective-permute-start(f32[1,18,1]{2,1,0:T(8,128)S(1)} %get-tuple-element.67), channel_id=1, source_target_pairs={{0,1},{1,2},{2,3},{3,0},{4,5},{5,6},{6,7},{7,4},{8,9},{9,10},{10,1... | collective-permute-start | bytes 224 | tf_op jit(solution)/shard_map/ppermute | solution.py:19
  64.0 5.5 %collective-permute-start.11 = (f32[1,18,1]{2,1,0:T(8,128)S(1)}, f32[1,18,1]{2,1,0:T(8,128)S(1)}, u32[]{:S(2)}, u32[]{:S(2)}) collective-permute-start(f32[1,18,1]{2,1,0:T(8,128)S(1)} %get-tuple-element.68), channel_id=1, source_target_pairs={{1,0},{2,1},{3,2},{0,3},{5,4},{6,5},{7,6},{4,7},{9,8},{10,9},{11,1... | collective-permute-start | bytes 224 | tf_op jit(solution)/shard_map/ppermute | solution.py:21
  70.8 4.6 %collective-permute-start.12 = (f32[1,1,128]{2,1,0:T(1,128)S(1)}, f32[1,1,128]{2,1,0:T(1,128)S(1)}, u32[]{:S(2)}, u32[]{:S(2)}) collective-permute-start(f32[1,1,128]{2,1,0:T(1,128)S(1)} %get-tuple-element.75), channel_id=1, source_target_pairs={{0,4},{4,8},{8,12},{1,5},{5,9},{9,13},{2,6},{6,10},{10,14},{3,7},{... | collective-permute-start | bytes 1544 | tf_op jit(solution)/shard_map/ppermute | solution.py:19
  74.1 3.5 %collective-permute-start.13 = (f32[1,1,128]{2,1,0:T(1,128)S(1)}, f32[1,1,128]{2,1,0:T(1,128)S(1)}, u32[]{:S(2)}, u32[]{:S(2)}) collective-permute-start(f32[1,1,128]{2,1,0:T(1,128)S(1)} %get-tuple-element.76), channel_id=1, source_target_pairs={{4,0},{8,4},{12,8},{5,1},{9,5},{13,9},{6,2},{10,6},{14,10},{7,3},{... | collective-permute-start | bytes 1544 | tf_op jit(solution)/shard_map/ppermute | solution.py:21
  77.7 5.5 %collective-permute-start.14 = (f32[1,18,1]{2,1,0:T(8,128)S(1)}, f32[1,18,1]{2,1,0:T(8,128)S(1)}, u32[]{:S(2)}, u32[]{:S(2)}) collective-permute-start(f32[1,18,1]{2,1,0:T(8,128)S(1)} %get-tuple-element.65), channel_id=1, source_target_pairs={{0,1},{1,2},{2,3},{3,0},{4,5},{5,6},{6,7},{7,4},{8,9},{9,10},{10,1... | collective-permute-start | bytes 224 | tf_op jit(solution)/shard_map/ppermute | solution.py:19
  78.8 4.4 %collective-permute-start.15 = (f32[1,18,1]{2,1,0:T(8,128)S(1)}, f32[1,18,1]{2,1,0:T(8,128)S(1)}, u32[]{:S(2)}, u32[]{:S(2)}) collective-permute-start(f32[1,18,1]{2,1,0:T(8,128)S(1)} %get-tuple-element.66), channel_id=1, source_target_pairs={{1,0},{2,1},{3,2},{0,3},{5,4},{6,5},{7,6},{4,7},{9,8},{10,9},{11,1... | collective-permute-start | bytes 224 | tf_op jit(solution)/shard_map/ppermute | solution.py:21
  84.6 4.7 %collective-permute-start.16 = (f32[1,1,128]{2,1,0:T(1,128)S(1)}, f32[1,1,128]{2,1,0:T(1,128)S(1)}, u32[]{:S(2)}, u32[]{:S(2)}) collective-permute-start(f32[1,1,128]{2,1,0:T(1,128)S(1)} %get-tuple-element.73), channel_id=1, source_target_pairs={{0,4},{4,8},{8,12},{1,5},{5,9},{9,13},{2,6},{6,10},{10,14},{3,7},{... | collective-permute-start | bytes 1544 | tf_op jit(solution)/shard_map/ppermute | solution.py:19
  88.0 3.5 %collective-permute-start.17 = (f32[1,1,128]{2,1,0:T(1,128)S(1)}, f32[1,1,128]{2,1,0:T(1,128)S(1)}, u32[]{:S(2)}, u32[]{:S(2)}) collective-permute-start(f32[1,1,128]{2,1,0:T(1,128)S(1)} %get-tuple-element.74), channel_id=1, source_target_pairs={{4,0},{8,4},{12,8},{5,1},{9,5},{13,9},{6,2},{10,6},{14,10},{7,3},{... | collective-permute-start | bytes 1544 | tf_op jit(solution)/shard_map/ppermute | solution.py:21
  91.5 5.5 %collective-permute-start.18 = (f32[1,18,1]{2,1,0:T(8,128)S(1)}, f32[1,18,1]{2,1,0:T(8,128)S(1)}, u32[]{:S(2)}, u32[]{:S(2)}) collective-permute-start(f32[1,18,1]{2,1,0:T(8,128)S(1)} %get-tuple-element.63), channel_id=1, source_target_pairs={{0,1},{1,2},{2,3},{3,0},{4,5},{5,6},{6,7},{7,4},{8,9},{9,10},{10,1... | collective-permute-start | bytes 224 | tf_op jit(solution)/shard_map/ppermute | solution.py:19
  92.8 4.2 %collective-permute-start.19 = (f32[1,18,1]{2,1,0:T(8,128)S(1)}, f32[1,18,1]{2,1,0:T(8,128)S(1)}, u32[]{:S(2)}, u32[]{:S(2)}) collective-permute-start(f32[1,18,1]{2,1,0:T(8,128)S(1)} %get-tuple-element.64), channel_id=1, source_target_pairs={{1,0},{2,1},{3,2},{0,3},{5,4},{6,5},{7,6},{4,7},{9,8},{10,9},{11,1... | collective-permute-start | bytes 224 | tf_op jit(solution)/shard_map/ppermute | solution.py:21
  98.3 9.5 %collective-permute-start.20 = (f32[1,1,128]{2,1,0:T(1,128)S(1)}, f32[1,1,128]{2,1,0:T(1,128)S(1)}, u32[]{:S(2)}, u32[]{:S(2)}) collective-permute-start(f32[1,1,128]{2,1,0:T(1,128)S(1)} %get-tuple-element.71), channel_id=1, source_target_pairs={{0,4},{4,8},{8,12},{1,5},{5,9},{9,13},{2,6},{6,10},{10,14},{3,7},{... | collective-permute-start | bytes 1544 | tf_op jit(solution)/shard_map/ppermute | solution.py:19
  101.7 6.1 %collective-permute-start.21 = (f32[1,1,128]{2,1,0:T(1,128)S(1)}, f32[1,1,128]{2,1,0:T(1,128)S(1)}, u32[]{:S(2)}, u32[]{:S(2)}) collective-permute-start(f32[1,1,128]{2,1,0:T(1,128)S(1)} %get-tuple-element.72), channel_id=1, source_target_pairs={{4,0},{8,4},{12,8},{5,1},{9,5},{13,9},{6,2},{10,6},{14,10},{7,3},{... | collective-permute-start | bytes 1544 | tf_op jit(solution)/shard_map/ppermute | solution.py:21
  103.0 14.8 %collective-permute-start.24 = (bf16[1,1,128,128]{3,2,1,0:T(8,128)(2,1)S(1)}, bf16[1,1,128,128]{3,2,1,0:T(8,128)(2,1)S(1)}, u32[]{:S(2)}, u32[]{:S(2)}) collective-permute-start(bf16[1,1,128,128]{3,2,1,0:T(8,128)(2,1)S(1)} %get-tuple-element.54), channel_id=1, source_target_pairs={{0,4},{4,8},{8,12},{1,5},{5,9},{9,13},{2,6},{6,10},{10,14},{3,7},{... | collective-permute-start | bytes 98312 | tf_op jit(solution)/shard_map/ppermute | solution.py:19
  106.4 11.4 %collective-permute-start.25 = (bf16[1,1,128,128]{3,2,1,0:T(8,128)(2,1)S(1)}, bf16[1,1,128,128]{3,2,1,0:T(8,128)(2,1)S(1)}, u32[]{:S(2)}, u32[]{:S(2)}) collective-permute-start(bf16[1,1,128,128]{3,2,1,0:T(8,128)(2,1)S(1)} %get-tuple-element.53), channel_id=1, source_target_pairs={{4,0},{8,4},{12,8},{5,1},{9,5},{13,9},{6,2},{10,6},{14,10},{7,3},{... | collective-permute-start | bytes 98312 | tf_op jit(solution)/shard_map/ppermute | solution.py:21
  107.9 5.5 %collective-permute-start.22 = (f32[1,18,1]{2,1,0:T(8,128)S(1)}, f32[1,18,1]{2,1,0:T(8,128)S(1)}, u32[]{:S(2)}, u32[]{:S(2)}) collective-permute-start(f32[1,18,1]{2,1,0:T(8,128)S(1)} %get-tuple-element.61), channel_id=1, source_target_pairs={{0,1},{1,2},{2,3},{3,0},{4,5},{5,6},{6,7},{7,4},{8,9},{9,10},{10,1... | collective-permute-start | bytes 224 | tf_op jit(solution)/shard_map/ppermute | solution.py:19
  109.2 4.2 %collective-permute-start.23 = (f32[1,18,1]{2,1,0:T(8,128)S(1)}, f32[1,18,1]{2,1,0:T(8,128)S(1)}, u32[]{:S(2)}, u32[]{:S(2)}) collective-permute-start(f32[1,18,1]{2,1,0:T(8,128)S(1)} %get-tuple-element.62), channel_id=1, source_target_pairs={{1,0},{2,1},{3,2},{0,3},{5,4},{6,5},{7,6},{4,7},{9,8},{10,9},{11,1... | collective-permute-start | bytes 224 | tf_op jit(solution)/shard_map/ppermute | solution.py:21
  117.8 4.4 %copy-start.1 = (bf16[3,3,128,128]{3,2,1,0:T(8,128)(2,1)S(1)}, bf16[3,3,128,128]{3,2,1,0:T(8,128)(2,1)}, u32[]{:S(2)}) copy-start(bf16[3,3,128,128]{3,2,1,0:T(8,128)(2,1)} %param.10) | copy-start | bytes 884740
  118.2 5.6 %collective-permute-start.26 = (bf16[1,18,1,128]{3,2,1,0:T(2,128)(2,1)S(1)}, bf16[1,18,1,128]{3,2,1,0:T(2,128)(2,1)S(1)}, u32[]{:S(2)}, u32[]{:S(2)}) collective-permute-start(bf16[1,18,1,128]{3,2,1,0:T(2,128)(2,1)S(1)} %get-tuple-element.44), channel_id=1, source_target_pairs={{0,1},{1,2},{2,3},{3,0},{4,5},{5,6},{6,7},{7,4},{8,9},{9,10},{10,1... | collective-permute-start | bytes 13832 | tf_op jit(solution)/shard_map/ppermute | solution.py:19
  119.6 4.2 %collective-permute-start.27 = (bf16[1,18,1,128]{3,2,1,0:T(2,128)(2,1)S(1)}, bf16[1,18,1,128]{3,2,1,0:T(2,128)(2,1)S(1)}, u32[]{:S(2)}, u32[]{:S(2)}) collective-permute-start(bf16[1,18,1,128]{3,2,1,0:T(2,128)(2,1)S(1)} %get-tuple-element.45), channel_id=1, source_target_pairs={{1,0},{2,1},{3,2},{0,3},{5,4},{6,5},{7,6},{4,7},{9,8},{10,9},{11,1... | collective-permute-start | bytes 13832 | tf_op jit(solution)/shard_map/ppermute | solution.py:21
  125.0 0.7 copy-start.4
  126.8 0.7 copy-start.5
  131.4 0.8 copy-start.2
  132.3 49.1 %collective-permute-start.28 = (bf16[1,1,128,128]{3,2,1,0:T(8,128)(2,1)S(1)}, bf16[1,1,128,128]{3,2,1,0:T(8,128)(2,1)S(1)}, u32[]{:S(2)}, u32[]{:S(2)}) collective-permute-start(bf16[1,1,128,128]{3,2,1,0:T(8,128)(2,1)S(1)} %get-tuple-element.48), channel_id=1, source_target_pairs={{0,4},{4,8},{8,12},{1,5},{5,9},{9,13},{2,6},{6,10},{10,14},{3,7},{... | collective-permute-start | bytes 98312 | tf_op jit(solution)/shard_map/ppermute | solution.py:19
  134.5 46.9 %collective-permute-start.29 = (bf16[1,1,128,128]{3,2,1,0:T(8,128)(2,1)S(1)}, bf16[1,1,128,128]{3,2,1,0:T(8,128)(2,1)S(1)}, u32[]{:S(2)}, u32[]{:S(2)}) collective-permute-start(bf16[1,1,128,128]{3,2,1,0:T(8,128)(2,1)S(1)} %get-tuple-element.49), channel_id=1, source_target_pairs={{4,0},{8,4},{12,8},{5,1},{9,5},{13,9},{6,2},{10,6},{14,10},{7,3},{... | collective-permute-start | bytes 98312 | tf_op jit(solution)/shard_map/ppermute | solution.py:21
  181.4 3.7 %collective-permute-start.30 = (bf16[1,18,1,128]{3,2,1,0:T(2,128)(2,1)S(1)}, bf16[1,18,1,128]{3,2,1,0:T(2,128)(2,1)S(1)}, u32[]{:S(2)}, u32[]{:S(2)}) collective-permute-start(bf16[1,18,1,128]{3,2,1,0:T(2,128)(2,1)S(1)} %get-tuple-element.39), channel_id=1, source_target_pairs={{1,0},{2,1},{3,2},{0,3},{5,4},{6,5},{7,6},{4,7},{9,8},{10,9},{11,1... | collective-permute-start | bytes 13832 | tf_op jit(solution)/shard_map/ppermute | solution.py:21
  183.7 5.5 %collective-permute-start.31 = (bf16[1,18,1,128]{3,2,1,0:T(2,128)(2,1)S(1)}, bf16[1,18,1,128]{3,2,1,0:T(2,128)(2,1)S(1)}, u32[]{:S(2)}, u32[]{:S(2)}) collective-permute-start(bf16[1,18,1,128]{3,2,1,0:T(2,128)(2,1)S(1)} %get-tuple-element.40), channel_id=1, source_target_pairs={{0,1},{1,2},{2,3},{3,0},{4,5},{5,6},{6,7},{7,4},{8,9},{9,10},{10,1... | collective-permute-start | bytes 13832 | tf_op jit(solution)/shard_map/ppermute | solution.py:19
Sparse Core Ops, SparseCore 0:
  132.4 58.1 reduce-scatter.1
